TPU v7x, 32 devices: a whole 2x2x4 slice. The times are simulated.
32 devices in a mesh: sky: 8 (over z, y), band: 4 (over x, core).
Axes of the slice: x: 2, y: 2, z: 4, core: 2. Of those that a mesh axis runs over, the one named last changes fastest.
Arguments:
- magnitudes: float32 [4, 8, 16384], P('band', None, 'sky'), may hold values from -7 to 7
- weights: float32 [4, 8, 16384], P('band', None, 'sky'), may hold values from 0.25 to 4
- slots: int32 [4, 8, 16384], P('band', None, 'sky'), may hold values from 0 to 31, as said below
- block_fields: int32 [64, 32], P('sky'), may hold values from 0 to 4096, as said below
- owner: int32 [4096], replicated, may hold values from 0 to 7, as said below
- colors: int32 [4096], replicated, may hold values from 0 to 7
- color_terms: float32 [4, 4], replicated, may hold values from -0.25 to 0.25
Outputs:
- zero_points: float32 [4, 4096], P('band', 'sky')
- star_mags: float32 [4, 16384], P('band', 'sky')
- misfit: float32 [4, 4], P(None, 'band')
Inputs may be any that keep to these rules, and one draw needn't show every extreme that they name: `block_fields`: the live entries of each list come first, are distinct, and name fields owned by the block's own sky tile or by the tiles one index below or above it, cyclically over 8 tiles; the remaining entries equal 4096. A list holds 16 or more live entries, and every tile has a block with all 32 live. `owner`: each sky tile owns exactly 512 fields. `slots`: each observation names a live entry of its block's list.
All inputs are finite; a program needn't handle non-finite values.
Results may differ from a plain program's by a relative error of at most 0.00023.
Values sent between devices are 32-bit elements; how exact they have to be, the bound alone decides.
A program may use at most 64 MiB of HBM per device.

v0:
```python
import functools

import jax
import jax.numpy as jnp
from jax import lax
from jax.experimental import pallas as pl
from jax.experimental.pallas import tpu as pltpu
from jax.sharding import PartitionSpec as P

COLORS = 8
SWEEPS = 4
PRIOR_WEIGHT = 1.0
REACH = 2
HIGHEST = lax.Precision.HIGHEST
LANES = 128
EXTRA = 8
MESH = pl.DeviceIdType.MESH


def contract_lanes(left, right):
    dims = (((1,), (1,)), ((), ()))
    return lax.dot_general(left, right, dims, precision=HIGHEST, preferred_element_type=jnp.float32)


def couple_kernel(bands, obs, list_len, rows, mix_ref, mix_grid_ref, data_ref, out_ref):
    blocks = data_ref.shape[2] // rows
    full = []
    entry = lax.broadcasted_iota(jnp.int32, (list_len, rows), 0).astype(jnp.float32)
    for block in range(blocks):
        cols = pl.ds(block * rows, rows)
        one_hot, one_hot_mag, star_weight, means = [], [], [], []
        for band in range(bands):
            mags = data_ref[band, 0:obs, cols]
            wts = data_ref[band, obs : 2 * obs, cols]
            slots = data_ref[band, 2 * obs : 3 * obs, cols]
            scaled = wts * mags
            weight_sum = jnp.sum(wts, axis=0, keepdims=True)
            star_weight.append(weight_sum)
            means.append(jnp.sum(scaled, axis=0, keepdims=True) / weight_sum)
            hot = jnp.zeros((list_len, rows), jnp.float32)
            hot_mag = jnp.zeros((list_len, rows), jnp.float32)
            for k in range(obs):
                hit = slots[k : k + 1] == entry
                hot = hot + jnp.where(hit, wts[k : k + 1], 0.0)
                hot_mag = hot_mag + jnp.where(hit, scaled[k : k + 1], 0.0)
            one_hot.append(hot)
            one_hot_mag.append(hot_mag)
        rest = []
        shares = []
        for band in range(bands):
            predicted = mix_ref[band, 0] * means[0]
            for other in range(1, bands):
                predicted = predicted + mix_ref[band, other] * means[other]
            rest.append(one_hot_mag[band] - one_hot[band] * predicted)
            shares.append(one_hot[band] / star_weight[band])
        hot_all = jnp.concatenate(one_hot, axis=0)
        share_all = jnp.concatenate(shares, axis=0)
        rest_all = jnp.concatenate(rest, axis=0)
        coupling = contract_lanes(share_all, hot_all) * mix_grid_ref[...]
        ones = jnp.ones((8, rows), jnp.float32)
        rest_row = contract_lanes(ones, rest_all)
        weight_row = contract_lanes(ones, hot_all)
        first = lax.broadcasted_iota(jnp.int32, (EXTRA, LANES), 0) == 0
        full.append(jnp.concatenate([coupling, jnp.where(first, rest_row, weight_row)], axis=0))
    split = bands // 2
    for part in range(split):
        pieces = []
        for half in range(2):
            band = half * split + part
            for block in range(blocks):
                pieces.append(full[block][:, band * list_len : (band + 1) * list_len])
        out_ref[part] = jnp.concatenate(pieces, axis=1)


def sweep_kernel(bands, list_len, row_count, coupled_ref, pick_ref, color_ref, out_ref, kt, base, tot, rden, zp, stage, sems):
    groups = row_count // 8
    pack = LANES // list_len
    split = bands // 2
    patterns = pick_ref.shape[0]
    depth = stage.shape[0]
    lane = lax.broadcasted_iota(jnp.int32, (8, LANES), 1)
    lane_wide = lax.broadcasted_iota(jnp.int32, (LANES + EXTRA, LANES), 1)

    def fetch(row, slot):
        return pltpu.make_async_copy(
            coupled_ref.at[pl.ds(row * (2 * split), 2 * split)], stage.at[slot], sems.at[slot]
        )

    for row in range(depth - 1):
        fetch(row, row).start()

    def unpack(row, carry):
        slot = lax.rem(row, depth)
        ahead = row + depth - 1

        @pl.when(ahead < row_count)
        def _():
            fetch(ahead, lax.rem(ahead, depth)).start()

        fetch(row, slot).wait()
        group = lax.div(row, 8)
        place = lax.rem(row, 8)
        for part in range(split):
            left = stage[slot, part]
            right = stage[slot, split + part]
            low = jnp.where(lane_wide < LANES // 2, left, pltpu.roll(right, LANES // 2, 1))
            high = jnp.where(lane_wide < LANES // 2, pltpu.roll(left, LANES // 2, 1), right)
            for band, value in ((part, low), (split + part, high)):
                start = (group * bands + band) * (LANES * 8) + place
                kt[pl.ds(start, LANES, stride=8), :] = value[0:LANES]
                base[band, pl.ds(row, 1), :] = value[LANES : LANES + 1]
                tot[band, pl.ds(row + 8, 1), :] = value[LANES + 1 : LANES + 2]
        return carry

    lax.fori_loop(0, row_count, unpack, 0)

    def rows_of(group):
        return pl.ds(pl.multiple_of(group * 8, 8), 8)

    def wrap():
        for band in range(bands):
            tot[band, 0:8, :] = tot[band, row_count : row_count + 8, :]
            tot[band, row_count + 8 : row_count + 16, :] = tot[band, 8:16, :]

    def take(value, picks):
        return jnp.take_along_axis(value, picks, axis=1, mode="promise_in_bounds")

    def gathered(group):
        sums = [jnp.zeros((8, LANES), jnp.float32) for _ in range(2 * bands)]
        for place in range(patterns // pack):
            start = group * 8 + (8 + place - patterns // pack // 2)
            near = [tot[band, pl.ds(start, 8), :] for band in range(bands)]
            for quarter in range(pack):
                pick = pick_ref[place * pack + quarter, rows_of(group), :]
                mask = pick < LANES
                lanes = pick & (LANES - 1)
                for band in range(bands):
                    index = 2 * band + quarter % 2
                    sums[index] = sums[index] + jnp.where(mask, take(near[band], lanes), 0.0)
        return [sums[2 * band] + sums[2 * band + 1] for band in range(bands)]

    def weigh(group, carry):
        for band, value in enumerate(gathered(group)):
            rden[band, rows_of(group), :] = 1.0 / (value + PRIOR_WEIGHT)
        return carry

    wrap()
    lax.fori_loop(0, groups, weigh, 0)
    zp[...] = jnp.zeros_like(zp)

    def step(number, carry):
        color_no = lax.rem(number, COLORS)

        def total(group, inner):
            here = [zp[band, rows_of(group), :] for band in range(bands)]
            sums = [base[band, rows_of(group), :] for band in range(bands)]
            for entry in range(list_len):
                lanes = (lane & (LANES - list_len)) + entry
                values = [take(here[band], lanes) for band in range(bands)]
                for band in range(bands):
                    for other in range(bands):
                        start = (group * bands + band) * (LANES * 8) + (other * list_len + entry) * 8
                        rows = pl.ds(pl.multiple_of(start, 8), 8)
                        sums[band] = sums[band] + values[other] * kt[rows, :]
            for band in range(bands):
                tot[band, pl.ds(pl.multiple_of(group * 8 + 8, 8), 8), :] = sums[band]
            return inner

        lax.fori_loop(0, groups, total, 0, unroll=2)
        wrap()

        def update(group, inner):
            rows = rows_of(group)
            now = color_ref[rows, :] == color_no
            for band, value in enumerate(gathered(group)):
                zp[band, rows, :] = jnp.where(now, value * rden[band, rows, :], zp[band, rows, :])
            return inner

        lax.fori_loop(0, groups, update, 0, unroll=2)

        @pl.when(color_no == COLORS - 1)
        def _():
            out_ref[lax.div(number, COLORS)] = zp[...]

        return carry

    lax.fori_loop(0, SWEEPS * COLORS, step, 0)


def greet(axes):
    barrier = pltpu.get_barrier_semaphore()
    total = 0
    for axis, count in axes:
        for step in range(1, count):
            peer = lax.rem(lax.axis_index(axis) + step, count)
            pl.semaphore_signal(barrier, inc=1, device_id={axis: peer}, device_id_type=MESH)
            total += 1
    pl.semaphore_wait(barrier, total)


def send_all(axis, count, source, target, send_sems, recv_sems, first):
    me = lax.axis_index(axis)
    copies = []
    for step in range(1, count):
        peer = lax.rem(me + step, count)
        copy = pltpu.make_async_remote_copy(
            src_ref=source(peer),
            dst_ref=target.at[me],
            send_sem=send_sems.at[first + step - 1],
            recv_sem=recv_sems.at[first + step - 1],
            device_id={axis: peer},
            device_id_type=MESH,
        )
        copy.start()
        copies.append(copy)
    return copies


def exchange_kernel(tiles, bands, lists_ref, own_ref, all_lists_ref, data_ref, send_sems, recv_sems):
    greet((("sky", tiles), ("band", bands)))
    copies = send_all("sky", tiles, lambda peer: lists_ref, all_lists_ref, send_sems, recv_sems, 0)
    copies += send_all("band", bands, lambda peer: own_ref.at[peer], data_ref, send_sems, recv_sems, tiles - 1)
    my_band = lax.axis_index("band")
    all_lists_ref[lax.axis_index("sky")] = lists_ref[...]
    data_ref[my_band] = own_ref[my_band]
    for copy in copies:
        copy.wait()


def spread_kernel(high_count, matching, own_ref, rows_ref, all_ref, pick_ref, send_sems, recv_sems):
    sky, band = lax.axis_index("sky"), lax.axis_index("band")
    high, low = sky // 2, sky % 2
    side, core = band // 2, band % 2
    highs = [lax.rem(high + step, high_count) for step in range(1, high_count)]
    to_low = {"sky": high * 2 + (1 - low)}
    to_side = {"band": (1 - side) * 2 + core}
    to_core = {"band": side * 2 + (1 - core)}
    peers = [{"sky": peer * 2 + low} for peer in highs] + [to_low, to_side, to_core]
    barrier = pltpu.get_barrier_semaphore()
    for peer in peers:
        pl.semaphore_signal(barrier, inc=1, device_id=peer, device_id_type=MESH)
    pl.semaphore_wait(barrier, len(peers))
    count = [0]

    def send(source, target, peer):
        copy = pltpu.make_async_remote_copy(
            src_ref=source,
            dst_ref=target,
            send_sem=send_sems.at[count[0]],
            recv_sem=recv_sems.at[count[0]],
            device_id=peer,
            device_id_type=MESH,
        )
        count[0] += 1
        copy.start()
        return copy

    def wait(copies):
        for copy in copies:
            copy.wait()

    mine = all_ref.at[high, low, side, core]
    copies = [send(own_ref, mine, peer) for peer in peers[: high_count - 1]]
    all_ref[high, low, side, core] = own_ref[...]
    match_kernel(*matching, rows_ref, pick_ref)
    wait(copies)

    column = all_ref.at[:, low, side, core]
    first = all_ref.at[:, low, side, core, 0]
    second = all_ref.at[:, low, side, core, 1]
    copies = [send(first, first, to_low), send(second, second, to_side)]
    late = [send(column, column, to_core)]
    wait(copies)

    first = all_ref.at[:, :, side, core, 0]
    second = all_ref.at[:, low, :, core, 1]
    copies = [send(first, first, to_side), send(second, second, to_low)]
    for part in (all_ref.at[:, 1 - low, side, core, 0], all_ref.at[:, low, 1 - side, core, 1]):
        late.append(send(part, part, to_core))
    wait(copies)

    for part in (all_ref.at[:, :, 1 - side, core, 0], all_ref.at[:, 1 - low, :, core, 1]):
        late.append(send(part, part, to_core))
    wait(late)


def total_kernel(tiles, bands, part_ref, out_ref, by_band, held, by_tile, send_sems, recv_sems):
    greet((("sky", tiles), ("band", bands)))
    copies = send_all("band", bands, lambda peer: part_ref, by_band, send_sems, recv_sems, tiles - 1)
    by_band[lax.axis_index("band")] = part_ref[...]
    for copy in copies:
        copy.wait()
    total = by_band[0]
    for band in range(1, bands):
        total = total + by_band[band]
    held[...] = total
    copies = send_all("sky", tiles, lambda peer: held, by_tile, send_sems, recv_sems, 0)
    by_tile[lax.axis_index("sky")] = total
    for copy in copies:
        copy.wait()
    total = by_tile[0]
    for tile in range(1, tiles):
        total = total + by_tile[tile]
    out_ref[...] = total


def match_kernel(list_len, fields, places, rows_ref, pick_ref):
    pack = LANES // list_len

    def group_picks(group, carry):
        home = rows_ref[pl.ds(pl.multiple_of(group * 8 + 8, 8), 8), :]
        home = jnp.where(home < fields, home, -1)
        near = [rows_ref[pl.ds(group * 8 + 8 + place - places // 2, 8), :] for place in range(places)]
        for quarter in range(pack):
            picks = [jnp.full((8, LANES), LANES, jnp.int32) for _ in range(places)]
            for entry in range(list_len):
                source = quarter * list_len + entry
                for place in range(places):
                    other = jnp.broadcast_to(near[place][:, source : source + 1], (8, LANES))
                    picks[place] = jnp.where(other == home, source, picks[place])
            for place in range(places):
                pick_ref[place * pack + quarter, pl.ds(pl.multiple_of(group * 8, 8), 8), :] = picks[place]
        return carry

    lax.fori_loop(0, pick_ref.shape[1] // 8, group_picks, 0)


def finish_kernel(bands, obs, list_len, rows, mix_ref, data_ref, own_ref, zp_two_ref, zp_own_ref, means_ref, misfit_ref):
    halves = rows // LANES
    pack = LANES // list_len
    mine = data_ref.shape[2] // rows
    first = lax.rem(lax.axis_index("band") * mine, pack)

    def spread(row, picks):
        table = jnp.broadcast_to(row, (obs, LANES))
        return jnp.take_along_axis(table, picks, axis=1, mode="promise_in_bounds")

    for block in range(zp_own_ref.shape[0] * pack):
        row = zp_own_ref[block // pack : block // pack + 1, :]
        for half in range(halves):
            cols = pl.ds(block * rows + half * LANES, LANES)
            wts = own_ref[obs : 2 * obs, cols]
            picks = own_ref[2 * obs : 3 * obs, cols].astype(jnp.int32) + block % pack * list_len
            left = wts * (own_ref[0:obs, cols] - spread(row, picks))
            means_ref[0:1, cols] = jnp.sum(left, axis=0, keepdims=True) / jnp.sum(wts, axis=0, keepdims=True)

    lines = []
    for sweep in range(SWEEPS):
        partial = [jnp.zeros((obs, LANES), jnp.float32) for _ in range(bands)]
        for block in range(mine):
            for half in range(halves):
                cols = pl.ds(block * rows + half * LANES, LANES)
                left, means = [], []
                for band in range(bands):
                    wts = data_ref[band, obs : 2 * obs, cols]
                    picks = data_ref[band, 2 * obs : 3 * obs, cols].astype(jnp.int32) + (first + block) * list_len
                    row = zp_two_ref[sweep, band]
                    mags = data_ref[band, 0:obs, cols] - spread(row, picks)
                    left.append(mags)
                    means.append(jnp.sum(wts * mags, axis=0, keepdims=True) / jnp.sum(wts, axis=0, keepdims=True))
                for band in range(bands):
                    predicted = mix_ref[band, 0] * means[0]
                    for other in range(1, bands):
                        predicted = predicted + mix_ref[band, other] * means[other]
                    wts = data_ref[band, obs : 2 * obs, cols]
                    partial[band] = partial[band] + wts * (left[band] - predicted) ** 2
        lines += [jnp.sum(partial[band], axis=0, keepdims=True) for band in range(bands)]
    lines.append(jnp.zeros((LANES - len(lines), LANES), jnp.float32))
    block_sums = jnp.concatenate(lines, axis=0)
    misfit_ref[...] = contract_lanes(jnp.ones((8, LANES), jnp.float32), block_sums)


def body(magnitudes, weights, slots, block_fields, owner, colors, color_terms):
    bands = color_terms.shape[0]
    tiles = lax.axis_size("sky")
    my_tile = lax.axis_index("sky")
    my_band = lax.axis_index("band")
    _, obs, stars = magnitudes.shape
    blocks, list_len = block_fields.shape
    rows = stars // blocks
    fields = owner.shape[0]
    owned = fields // tiles
    mine = blocks // bands
    pack = LANES // list_len
    tile_rows = blocks // pack
    row_count = tiles * tile_rows
    mixing = (
        jnp.eye(bands, dtype=jnp.float32) + color_terms - jnp.diag(jnp.sum(color_terms, axis=1))
    )
    vmem = pl.BlockSpec(memory_space=pltpu.VMEM)
    smem = pl.BlockSpec(memory_space=pltpu.SMEM)
    hbm = pl.BlockSpec(memory_space=pl.ANY)

    field_no = jnp.arange(fields, dtype=jnp.int32)[:, None]
    flat_fields = block_fields.reshape(1, -1)
    own_colors = jnp.sum(jnp.where(field_no == flat_fields, colors[:, None], 0), axis=0)
    own_colors = jnp.where(flat_fields[0] < fields, own_colors, -1)
    lists = jnp.stack([flat_fields[0], own_colors]).reshape(2 * tile_rows, LANES)
    own = jnp.concatenate([magnitudes[0], weights[0], slots[0].astype(jnp.float32)], axis=0)
    by_peer = own.reshape(3 * obs, bands, mine * rows).transpose(1, 0, 2)
    peers = tiles + bands - 2
    lists, data = pl.pallas_call(
        functools.partial(exchange_kernel, tiles, bands),
        out_shape=(
            jax.ShapeDtypeStruct((tiles,) + lists.shape, jnp.int32),
            jax.ShapeDtypeStruct(by_peer.shape, jnp.float32),
        ),
        in_specs=[vmem, vmem],
        out_specs=(vmem, vmem),
        scratch_shapes=[pltpu.SemaphoreType.DMA((peers,)), pltpu.SemaphoreType.DMA((peers,))],
        compiler_params=pltpu.CompilerParams(collective_id=0, has_side_effects=True),
        name="exchange",
    )(lists, by_peer)
    lists = lists.reshape(tiles, 2, tile_rows, LANES)
    all_fields = lists[:, 0].reshape(row_count, LANES)
    entry_colors = lists[:, 1].reshape(row_count, LANES)

    mix_grid = jnp.repeat(jnp.repeat(mixing.T, list_len, axis=0), list_len, axis=1)
    coupled = pl.pallas_call(
        functools.partial(couple_kernel, bands, obs, list_len, rows),
        out_shape=jax.ShapeDtypeStruct((bands // 2, LANES + EXTRA, LANES), jnp.float32),
        in_specs=[smem, vmem, vmem],
        out_specs=vmem,
        name="couple",
    )(mixing, mix_grid, data)
    reach_rows = REACH * tile_rows + tile_rows - 1
    padded = jnp.concatenate([all_fields[-8:], all_fields, all_fields[:8]], axis=0)
    places = 2 * reach_rows + 1
    everyone = (tiles // 2, 2, bands // 2, 2) + coupled.shape
    copies = tiles // 2 - 1 + 9
    coupled, pick = pl.pallas_call(
        functools.partial(spread_kernel, tiles // 2, (list_len, fields, places)),
        out_shape=(
            jax.ShapeDtypeStruct(everyone, jnp.float32),
            jax.ShapeDtypeStruct((places * pack, row_count, LANES), jnp.int32),
        ),
        in_specs=[vmem, vmem],
        out_specs=(vmem, vmem),
        scratch_shapes=[pltpu.SemaphoreType.DMA((copies,)), pltpu.SemaphoreType.DMA((copies,))],
        compiler_params=pltpu.CompilerParams(
            collective_id=2, has_side_effects=True, vmem_limit_bytes=60 * 1024 * 1024
        ),
        name="spread",
    )(coupled, padded)
    coupled = coupled.reshape((-1,) + coupled.shape[-2:])

    big = (bands, row_count, LANES)
    snapshots = pl.pallas_call(
        functools.partial(sweep_kernel, bands, list_len, row_count),
        out_shape=jax.ShapeDtypeStruct((SWEEPS,) + big, jnp.float32),
        in_specs=[hbm, vmem, vmem],
        out_specs=vmem,
        scratch_shapes=[
            pltpu.VMEM((row_count * bands * LANES, LANES), jnp.float32),
            pltpu.VMEM(big, jnp.float32),
            pltpu.VMEM((bands, row_count + 16, LANES), jnp.float32),
            pltpu.VMEM(big, jnp.float32),
            pltpu.VMEM(big, jnp.float32),
            pltpu.VMEM((4, bands, LANES + EXTRA, LANES), jnp.float32),
            pltpu.SemaphoreType.DMA((4,)),
        ],
        compiler_params=pltpu.CompilerParams(vmem_limit_bytes=60 * 1024 * 1024),
        name="sweeps",
    )(coupled, pick, entry_colors)

    final = lax.dynamic_index_in_dim(snapshots[SWEEPS - 1], my_band, 0, keepdims=False)
    zp_tile = lax.dynamic_slice_in_dim(final, my_tile * tile_rows, tile_rows, axis=0)
    my_row = (my_tile * blocks + my_band * mine) // pack
    zp_two = lax.dynamic_slice_in_dim(snapshots, my_row, 1, axis=2)
    star_means, partial = pl.pallas_call(
        functools.partial(finish_kernel, bands, obs, list_len, rows),
        out_shape=(
            jax.ShapeDtypeStruct((1, stars), jnp.float32),
            jax.ShapeDtypeStruct((8, LANES), jnp.float32),
        ),
        in_specs=[smem, vmem, vmem, vmem, vmem],
        out_specs=(vmem, vmem),
        name="finish",
    )(mixing, data, own, zp_two, zp_tile)
    slab = (8, LANES)
    total = pl.pallas_call(
        functools.partial(total_kernel, tiles, bands),
        out_shape=jax.ShapeDtypeStruct(slab, jnp.float32),
        in_specs=[vmem],
        out_specs=vmem,
        scratch_shapes=[
            pltpu.VMEM((bands,) + slab, jnp.float32),
            pltpu.VMEM(slab, jnp.float32),
            pltpu.VMEM((tiles,) + slab, jnp.float32),
            pltpu.SemaphoreType.DMA((peers,)),
            pltpu.SemaphoreType.DMA((peers,)),
        ],
        compiler_params=pltpu.CompilerParams(collective_id=1, has_side_effects=True),
        name="total",
    )(partial)
    misfit = total[0, : SWEEPS * bands].reshape(SWEEPS, bands) / (obs * stars * tiles)
    misfit = lax.dynamic_slice_in_dim(misfit, my_band, 1, axis=1)

    tile_ids = jnp.mod(my_tile + jnp.arange(3, dtype=jnp.int32) - 1, tiles)

    def close(table):
        by_tile = table.reshape(tiles, tile_rows * LANES)
        parts = [lax.dynamic_index_in_dim(by_tile, tile_ids[n], 0, keepdims=False) for n in range(3)]
        return jnp.concatenate(parts)

    close_fields = close(all_fields)
    is_mine = (owner == my_tile)[:, None]
    rank = jnp.sum((is_mine & (field_no < close_fields[None])).astype(jnp.int32), axis=0)
    has = jnp.sum((is_mine & (field_no == close_fields[None])).astype(jnp.int32), axis=0) > 0
    rank = jnp.where(has, rank, owned)
    entry_no = jnp.arange(close_fields.shape[0], dtype=jnp.int32)[:, None]
    hit = rank[:, None] == jnp.arange(owned, dtype=jnp.int32)[None]
    chosen = jnp.max(jnp.where(hit, entry_no, -1), axis=0)
    own_zp = jnp.sum(jnp.where(chosen[None] == entry_no, close(final)[:, None], 0.0), axis=0)
    return own_zp[None], star_means, misfit


def solution(mesh):
    in_specs = (
        P("band", None, "sky"),
        P("band", None, "sky"),
        P("band", None, "sky"),
        P("sky", None),
        P(),
        P(),
        P(),
    )
    out_specs = (P("band", "sky"), P("band", "sky"), P(None, "band"))
    return jax.shard_map(body, mesh=mesh, in_specs=in_specs, out_specs=out_specs, check_vma=False)
```

profile of v0, /device:TPU:0, one launch (start us, length us, event | category | flops | bytes accessed | tf_op | source)
XLA Modules:
  0.0 146.0 jit_solution(15773913396166607153)
XLA Ops:
  0.6 0.8 reduce_sum.51
  1.4 1.3 select_subtract_fusion.mix_ref
  2.8 0.8 fusion.6
  3.5 0.1 broadcast_in_dim.92
  3.6 0.1 reshape.74
  3.7 0.7 copy.23.mix_grid_ref
  4.4 0.8 eq.73
  5.2 2.5 %select_reduce_fusion = s32[256]{0:T(256)S(1)} fusion(s32[4096]{0:T(1024)} %param.12, s32[256]{0:T(256)S(1)} %eq.73), kind=kLoop, calls=%fused_computation.6 | loop fusion | flops 3145472 | bytes 18432 | tf_op jit(solution)/shard_map/reduce_sum | solution.py:396
  7.6 0.8 stack_squeeze_reshape.3
  8.4 0.6 reshape.72.lists_ref
  9.0 0.8 convert_bitcast_fusion
  9.9 0.0 copy-start.2
  9.9 1.6 %maximum_bitcast_fusion.own_ref = f32[4,24,512]{2,1,0:T(8,128)} fusion(f32[8,4,512]{2,0,1:T(8,128)S(1)} %bitcast.51, f32[8,4,512]{2,0,1:T(8,128)} %bitcast.53, f32[8,4,512]{2,0,1:T(8,128)} %bitcast.55), kind=kLoop, calls=%fused_computation.12 | loop fusion | flops 98304 | bytes 393216 | tf_op jit(solution)/shard_map/transpose | solution.py:400
  11.4 0.0 copy-start
  11.5 0.0 copy-start.1
  11.5 11.4 %exchange.1 = (s32[8,4,128]{2,1,0:T(4,128)}, f32[4,24,512]{2,1,0:T(8,128)}) custom-call(s32[4,128]{1,0:T(4,128)} %reshape.72.lists_ref, f32[4,24,512]{2,1,0:T(8,128)} %maximum_bitcast_fusion.own_ref), custom_call_target="tpu_custom_call" | custom-call | tf_op jit(solution)/shard_map/exchange/pallas_call | solution.py:402
  22.9 2.8 %couple.1.own_ref = f32[2,136,128]{2,1,0:T(8,128)} custom-call(f32[4,4]{1,0:T(4,128)} %select_subtract_fusion.mix_ref, f32[128,128]{1,0:T(8,128)} %copy.23.mix_grid_ref, f32[4,24,512]{2,1,0:T(8,128)} %get-tuple-element.10.data_ref), custom_call_target="tpu_custom_call" | custom-call | tf_op jit(solution)/shard_map/couple/pallas_call | solution.py:419
  25.7 0.7 fusion.4
  26.4 1.3 slice_bitcast_fusion
  27.7 0.6 pad_add_fusion.rows_ref
  28.3 37.9 %spread.1 = (f32[4,2,2,2,2,136,128]{6,5,4,3,2,1,0:T(8,128)}, s32[44,16,128]{2,1,0:T(8,128)}) custom-call(f32[2,136,128]{2,1,0:T(8,128)} %couple.1.own_ref, s32[32,128]{1,0:T(8,128)} %pad_add_fusion.rows_ref), custom_call_target="tpu_custom_call" | custom-call | tf_op jit(solution)/shard_map/spread/pallas_call | solution.py:431
  66.2 48.5 %sweeps.1 = f32[4,4,16,128]{3,2,1,0:T(8,128)} custom-call(f32[64,136,128]{2,1,0:T(8,128)} %bitcast.50, s32[44,16,128]{2,1,0:T(8,128)} %get-tuple-element.12.pick_ref, s32[16,128]{1,0:T(8,128)} %bitcast.59), custom_call_target="tpu_custom_call" | custom-call | tf_op jit(solution)/shard_map/sweeps/pallas_call | solution.py:448
  114.7 0.8 slice.53
  115.4 0.6 fusion.5
  121.9 0.0 copy-done.2
  122.0 4.1 %convert_reduce_fusion.1 = (s32[768]{0:T(1024)S(1)}, s32[768]{0:T(1024)S(1)}) fusion(s32[768]{0:T(1024)S(1)} %pad_add_fusion.1, pred[4096]{0:T(1024)(128)(4,1)S(1)} %broadcast_compare_fusion), kind=kLoop, calls=%fused_computation.2 | loop fusion | flops 25164288 | bytes 13312 | tf_op jit(solution)/shard_map/reduce_sum | solution.py:509
  126.1 0.3 select_reduce_fusion.2
  126.4 0.9 select_reduce_fusion.1
  127.2 0.0 copy-done
  127.2 0.0 copy-done.1
  127.2 0.7 pad_maximum_fusion.own_ref
  127.9 1.4 constant_dynamic-slice_fusion.2.zp_two_ref
  129.4 0.5 fusion.2.zp_own_ref
  129.9 2.0 %finish.1 = (f32[1,2048]{1,0:T(1,128)}, f32[8,128]{1,0:T(8,128)}) custom-call(f32[4,4]{1,0:T(4,128)} %select_subtract_fusion.mix_ref, f32[4,24,512]{2,1,0:T(8,128)} %get-tuple-element.10.data_ref, f32[24,2048]{1,0:T(8,128)} %pad_maximum_fusion.own_ref, f32[4,4,1,128]{3,2,1,0:T(1,128)} %constant_dynamic-slice_fusion.2.zp_two_ref, f32[2,128]{1,0:T(2,128)} %fusion.2.zp_own_ref), custom_call_target="tpu_custom_call" | custom-call | tf_op jit(solution)/shard_map/finish/pallas_call | solution.py:470
  131.9 12.6 %total.1 = f32[8,128]{1,0:T(8,128)} custom-call(f32[8,128]{1,0:T(8,128)} %get-tuple-element.14.part_ref), custom_call_target="tpu_custom_call" | custom-call | tf_op jit(solution)/shard_map/total/pallas_call | solution.py:481
  144.6 0.7 multiply_reduce_fusion
  145.3 0.1 div.17
  145.3 0.1 constant_dynamic-slice_fusion
  145.4 0.6 copy.27
  (13 shorter events, 0.1 us)
Async XLA Ops:
  9.9 112.1 %copy-start.2 = (s32[4096]{0:T(1024)S(1)}, s32[4096]{0:T(1024)}, u32[]{:S(2)}) copy-start(s32[4096]{0:T(1024)} %param.11) | copy-start | bytes 49156
  11.4 115.8 %copy-start = (f32[1,8,2048]{2,1,0:T(8,128)S(1)}, f32[1,8,2048]{2,1,0:T(8,128)}, u32[]{:S(2)}) copy-start(f32[1,8,2048]{2,1,0:T(8,128)} %param.8) | copy-start | bytes 196612
  11.5 115.8 %copy-start.1 = (f32[1,8,2048]{2,1,0:T(8,128)S(1)}, f32[1,8,2048]{2,1,0:T(8,128)}, u32[]{:S(2)}) copy-start(f32[1,8,2048]{2,1,0:T(8,128)} %param.7) | copy-start | bytes 196612
where the time goes:
time: 147 us; the launch traced here: 146 us
  Pallas kernels  115 us (78%)
  other arithmetic  15.1 us (10%)
  local copies, waits for them, and re-layouts  9.13 us (6%)
  between operations  6.58 us (4%)
    pallas_call x1, Pallas kernels, body(): pl.pallas_call(functools.partial(sweep_kernel, bands, list_len, row_count...  48.5 us
    pallas_call x1, Pallas kernels, body(): pl.pallas_call(functools.partial(spread_kernel, tiles // 2, (list_len, fi...  37.9 us
    pallas_call x1, Pallas kernels, body(): pl.pallas_call(functools.partial(total_kernel, tiles, bands), out_shape=j...  12.6 us
    pallas_call x1, Pallas kernels, body(): pl.pallas_call(functools.partial(exchange_kernel, tiles, bands), out_shap...  11.4 us
    reduce_sum x1, other arithmetic, body(): jnp.sum((is_mine & (field_no == close_fields[None])).astype(jnp.int32), a...  4.08 us

commit v1 on v0

--- a/solution.py
+++ b/solution.py
@@ -22,17 +22,17 @@
     return lax.dot_general(left, right, dims, precision=HIGHEST, preferred_element_type=jnp.float32)
 
 
-def couple_kernel(bands, obs, list_len, rows, mix_ref, mix_grid_ref, data_ref, out_ref):
-    blocks = data_ref.shape[2] // rows
+def couple_kernel(bands, obs, list_len, rows, mix_ref, mix_grid_ref, data_ref, places_ref, out_ref):
+    blocks = data_ref.shape[3] // rows
     full = []
-    entry = lax.broadcasted_iota(jnp.int32, (list_len, rows), 0).astype(jnp.float32)
+    entry = lax.broadcasted_iota(jnp.int32, (list_len, rows), 0)
     for block in range(blocks):
         cols = pl.ds(block * rows, rows)
         one_hot, one_hot_mag, star_weight, means = [], [], [], []
         for band in range(bands):
-            mags = data_ref[band, 0:obs, cols]
-            wts = data_ref[band, obs : 2 * obs, cols]
-            slots = data_ref[band, 2 * obs : 3 * obs, cols]
+            mags = data_ref[band, 0, :, cols]
+            wts = data_ref[band, 1, :, cols]
+            slots = places_ref[band, :, cols]
             scaled = wts * mags
             weight_sum = jnp.sum(wts, axis=0, keepdims=True)
             star_weight.append(weight_sum)
@@ -72,11 +72,15 @@
         out_ref[part] = jnp.concatenate(pieces, axis=1)
 
 
-def sweep_kernel(bands, list_len, row_count, coupled_ref, pick_ref, color_ref, out_ref, kt, base, tot, rden, zp, stage, sems):
+def sweep_kernel(
+    bands, list_len, row_count,
+    coupled_ref, pick_ref, color_ref,
+    out_ref, kt, base, tot, rden, zp, move, stage, sems, window,
+):
     groups = row_count // 8
     pack = LANES // list_len
     split = bands // 2
-    patterns = pick_ref.shape[0]
+    levels, places = pick_ref.shape[:2]
     depth = stage.shape[0]
     lane = lax.broadcasted_iota(jnp.int32, (8, LANES), 1)
     lane_wide = lax.broadcasted_iota(jnp.int32, (LANES + EXTRA, LANES), 1)
@@ -122,22 +126,46 @@
             tot[band, 0:8, :] = tot[band, row_count : row_count + 8, :]
             tot[band, row_count + 8 : row_count + 16, :] = tot[band, 8:16, :]
 
-    def take(value, picks):
-        return jnp.take_along_axis(value, picks, axis=1, mode="promise_in_bounds")
-
-    def gathered(group):
-        sums = [jnp.zeros((8, LANES), jnp.float32) for _ in range(2 * bands)]
-        for place in range(patterns // pack):
-            start = group * 8 + (8 + place - patterns // pack // 2)
+    def gather(group, first, count, sums):
+        for place in range(places):
+            start = group * 8 + (8 + place - places // 2)
             near = [tot[band, pl.ds(start, 8), :] for band in range(bands)]
-            for quarter in range(pack):
-                pick = pick_ref[place * pack + quarter, rows_of(group), :]
+            for level in range(count):
+                pick = pick_ref[first + level, place, rows_of(group), :]
                 mask = pick < LANES
                 lanes = pick & (LANES - 1)
                 for band in range(bands):
-                    index = 2 * band + quarter % 2
+                    index = 2 * band + level % 2
                     sums[index] = sums[index] + jnp.where(mask, take(near[band], lanes), 0.0)
+        return sums
+
+    def gathered(group):
+        sums = []
+        for band in range(bands):
+            sums += [tot[band, pl.ds(pl.multiple_of(group * 8 + 8, 8), 8), :], jnp.zeros((8, LANES), jnp.float32)]
+        sums = gather(group, 0, 2, sums)
+        sums = lax.fori_loop(2, window[2 * COLORS], lambda level, sums: gather(group, level, 1, sums), sums)
         return [sums[2 * band] + sums[2 * band + 1] for band in range(bands)]
+
+    position = (lane & (list_len - 1)).astype(jnp.float32)
+    for color_no in range(COLORS):
+        low = jnp.full((8, LANES), float(list_len), jnp.float32)
+        high = jnp.zeros((8, LANES), jnp.float32)
+        for group in range(groups):
+            now = color_ref[group * 8 : group * 8 + 8, :] == color_no
+            low = jnp.minimum(low, jnp.where(now, position, float(list_len)))
+            high = jnp.maximum(high, jnp.where(now, position + 1.0, 0.0))
+        window[2 * color_no] = jnp.min(low).astype(jnp.int32)
+        window[2 * color_no + 1] = jnp.max(high).astype(jnp.int32)
+    deepest = jnp.int32(2)
+    for level in range(2, levels):
+        def least(index, value, level=level):
+            place, group = lax.div(index, groups), lax.rem(index, groups)
+            return jnp.minimum(value, pick_ref[level, place, rows_of(group), :])
+        found = lax.fori_loop(0, places * groups, least, jnp.full((8, LANES), LANES, jnp.int32))
+        some = jnp.min(found.astype(jnp.float32)) < LANES
+        deepest = jnp.where(some, level + 1, deepest)
+    window[2 * COLORS] = deepest
 
     def weigh(group, carry):
         for band, value in enumerate(gathered(group)):
@@ -147,33 +175,39 @@
     wrap()
     lax.fori_loop(0, groups, weigh, 0)
     zp[...] = jnp.zeros_like(zp)
-
-    def step(number, carry):
-        color_no = lax.rem(number, COLORS)
-
-        def total(group, inner):
-            here = [zp[band, rows_of(group), :] for band in range(bands)]
-            sums = [base[band, rows_of(group), :] for band in range(bands)]
-            for entry in range(list_len):
-                lanes = (lane & (LANES - list_len)) + entry
+    tot[:, 8 : row_count + 8, :] = base[...]
+    wrap()
+
+    def push(width, origin):
+        def add(group, inner):
+            here = [move[band, rows_of(group), :] for band in range(bands)]
+            middle = pl.ds(pl.multiple_of(group * 8 + 8, 8), 8)
+            sums = [tot[band, middle, :] for band in range(bands)]
+            for entry in range(width):
+                lanes = (lane & (LANES - list_len)) + (origin + entry)
                 values = [take(here[band], lanes) for band in range(bands)]
                 for band in range(bands):
                     for other in range(bands):
-                        start = (group * bands + band) * (LANES * 8) + (other * list_len + entry) * 8
+                        start = (group * bands + band) * (LANES * 8) + (other * list_len + origin + entry) * 8
                         rows = pl.ds(pl.multiple_of(start, 8), 8)
                         sums[band] = sums[band] + values[other] * kt[rows, :]
             for band in range(bands):
-                tot[band, pl.ds(pl.multiple_of(group * 8 + 8, 8), 8), :] = sums[band]
+                tot[band, middle, :] = sums[band]
             return inner
 
-        lax.fori_loop(0, groups, total, 0, unroll=2)
-        wrap()
+        lax.fori_loop(0, groups, add, 0, unroll=2)
+
+    def step(number, carry):
+        color_no = lax.rem(number, COLORS)
 
         def update(group, inner):
             rows = rows_of(group)
             now = color_ref[rows, :] == color_no
             for band, value in enumerate(gathered(group)):
-                zp[band, rows, :] = jnp.where(now, value * rden[band, rows, :], zp[band, rows, :])
+                old = zp[band, rows, :]
+                new = jnp.where(now, value * rden[band, rows, :], old)
+                zp[band, rows, :] = new
+                move[band, rows, :] = new - old
             return inner
 
         lax.fori_loop(0, groups, update, 0, unroll=2)
@@ -182,6 +216,22 @@
         def _():
             out_ref[lax.div(number, COLORS)] = zp[...]
 
+        low, high = window[2 * color_no], window[2 * color_no + 1]
+        widths = (list_len // 4, list_len * 3 // 8, list_len // 2)
+        for index, width in enumerate(widths):
+            fits = high - low <= width
+            if index:
+                fits = fits & (high - low > widths[index - 1])
+
+            @pl.when(fits)
+            def _(width=width):
+                push(width, jnp.minimum(low, list_len - width))
+
+        @pl.when(high - low > widths[-1])
+        def _():
+            lax.fori_loop(0, 2, lambda part, inner: (push(widths[-1], part * widths[-1]), inner)[1], 0)
+
+        wrap()
         return carry
 
     lax.fori_loop(0, SWEEPS * COLORS, step, 0)
@@ -216,13 +266,109 @@
     return copies
 
 
-def exchange_kernel(tiles, bands, lists_ref, own_ref, all_lists_ref, data_ref, send_sems, recv_sems):
+def take(value, picks):
+    return jnp.take_along_axis(value, picks, axis=1, mode="promise_in_bounds")
+
+
+def sort_entries(list_len, fields, listed, color_ref):
+    lane = lax.broadcasted_iota(jnp.int32, (8, LANES), 1)
+    segment = lane & (LANES - list_len)
+    live = listed < fields
+    row_no, lane_no = listed // LANES, listed % LANES
+    color = jnp.full((8, LANES), -1, jnp.int32)
+    for row in range(color_ref.shape[0]):
+        table = jnp.broadcast_to(color_ref[row : row + 1, :], (8, LANES))
+        color = jnp.where(row_no == row, take(table, lane_no), color)
+    color = jnp.where(live, color, -1)
+    masks = jnp.concatenate([(color == c).astype(jnp.float32) for c in range(COLORS)], axis=0)
+    source = lax.broadcasted_iota(jnp.int32, (LANES, LANES), 0)
+    target = lax.broadcasted_iota(jnp.int32, (LANES, LANES), 1)
+    same = (source // list_len) == (target // list_len)
+    dims = (((1,), (0,)), ((), ()))
+    before = (same & (source < target)).astype(jnp.float32)
+    ranks = lax.dot_general(masks, before, dims, preferred_element_type=jnp.float32)
+    counts = lax.dot_general(masks, same.astype(jnp.float32), dims, preferred_element_type=jnp.float32)
+    rest = jnp.zeros((8, LANES), jnp.float32)
+    room = [None] * COLORS
+    for c in reversed(range(COLORS)):
+        rest = rest + counts[c * 8 : c * 8 + 8]
+        room[c] = list_len - rest
+    end = jnp.zeros((8, LANES), jnp.float32)
+    place = jnp.full((8, LANES), -1.0, jnp.float32)
+    for c in range(COLORS):
+        start = jnp.minimum(jnp.maximum(end, float(list_len * c // COLORS)), room[c])
+        end = start + counts[c * 8 : c * 8 + 8]
+        place = jnp.where(color == c, start + ranks[c * 8 : c * 8 + 8], place)
+    place = place.astype(jnp.int32)
+    sorted_fields = jnp.full((8, LANES), fields, jnp.int32)
+    sorted_colors = jnp.full((8, LANES), -1, jnp.int32)
+    for entry in range(list_len):
+        picks = segment + entry
+        hit = take(place, picks) == lane - segment
+        sorted_fields = jnp.where(hit, take(listed, picks), sorted_fields)
+        sorted_colors = jnp.where(hit, take(color, picks), sorted_colors)
+    return place, sorted_fields, sorted_colors
+
+
+def exchange_kernel(
+    tiles, bands, list_len, fields,
+    lists_ref, color_ref, mags_ref, wts_ref, slots_ref,
+    all_lists_ref, data_ref, places_ref, data_places_ref,
+    listed_ref, sorted_ref, send_sems, recv_sems,
+):
+    blocks = lists_ref.shape[0]
+    pack = LANES // list_len
+    tile_rows = blocks // pack
+    obs, stars = mags_ref.shape
+    rows = stars // blocks
+    mine = stars // bands
+    my_tile, my_band = lax.axis_index("sky"), lax.axis_index("band")
     greet((("sky", tiles), ("band", bands)))
-    copies = send_all("sky", tiles, lambda peer: lists_ref, all_lists_ref, send_sems, recv_sems, 0)
-    copies += send_all("band", bands, lambda peer: own_ref.at[peer], data_ref, send_sems, recv_sems, tiles - 1)
-    my_band = lax.axis_index("band")
-    all_lists_ref[lax.axis_index("sky")] = lists_ref[...]
-    data_ref[my_band] = own_ref[my_band]
+
+    def columns(band):
+        return pl.ds(pl.multiple_of(band * mine, LANES), mine)
+
+    count = [0]
+
+    def send(source, target, device):
+        copy = pltpu.make_async_remote_copy(
+            src_ref=source,
+            dst_ref=target,
+            send_sem=send_sems.at[count[0]],
+            recv_sem=recv_sems.at[count[0]],
+            device_id=device,
+            device_id_type=MESH,
+        )
+        count[0] += 1
+        copy.start()
+        return copy
+
+    peers = [lax.rem(my_band + step, bands) for step in range(1, bands)]
+    copies = []
+    for peer in peers:
+        copies.append(send(mags_ref.at[:, columns(peer)], data_ref.at[my_band, 0], {"band": peer}))
+        copies.append(send(wts_ref.at[:, columns(peer)], data_ref.at[my_band, 1], {"band": peer}))
+    listed_ref[...] = jnp.full((8, LANES), fields, jnp.int32)
+    for row in range(tile_rows):
+        pieces = [lists_ref[row * pack + part : row * pack + part + 1, :] for part in range(pack)]
+        listed_ref[row : row + 1, :] = jnp.concatenate(pieces, axis=1)
+    place, sorted_fields, sorted_colors = sort_entries(list_len, fields, listed_ref[...], color_ref)
+    sorted_ref[0] = sorted_fields[0:tile_rows]
+    sorted_ref[1] = sorted_colors[0:tile_rows]
+    for block in range(blocks):
+        table = jnp.broadcast_to(place[block // pack : block // pack + 1, :], (obs, LANES))
+        for half in range(rows // LANES):
+            cols = pl.ds(block * rows + half * LANES, LANES)
+            places_ref[:, cols] = take(table, slots_ref[:, cols] + block % pack * list_len)
+    for peer in peers:
+        copies.append(send(places_ref.at[:, columns(peer)], data_places_ref.at[my_band], {"band": peer}))
+    for step in range(1, tiles):
+        peer = lax.rem(my_tile + step, tiles)
+        copies.append(send(sorted_ref, all_lists_ref.at[my_tile], {"sky": peer}))
+    all_lists_ref[my_tile] = sorted_ref[...]
+    data_ref[my_band, 0] = mags_ref[:, columns(my_band)]
+    data_ref[my_band, 1] = wts_ref[:, columns(my_band)]
+    data_places_ref[my_band] = places_ref[:, columns(my_band)]
     for copy in copies:
         copy.wait()
 
@@ -306,11 +452,13 @@
 
 def match_kernel(list_len, fields, places, rows_ref, pick_ref):
     pack = LANES // list_len
+    lane = lax.broadcasted_iota(jnp.int32, (8, LANES), 1)
 
     def group_picks(group, carry):
         home = rows_ref[pl.ds(pl.multiple_of(group * 8 + 8, 8), 8), :]
         home = jnp.where(home < fields, home, -1)
         near = [rows_ref[pl.ds(group * 8 + 8 + place - places // 2, 8), :] for place in range(places)]
+        found = [[] for _ in range(places)]
         for quarter in range(pack):
             picks = [jnp.full((8, LANES), LANES, jnp.int32) for _ in range(places)]
             for entry in range(list_len):
@@ -319,29 +467,43 @@
                     other = jnp.broadcast_to(near[place][:, source : source + 1], (8, LANES))
                     picks[place] = jnp.where(other == home, source, picks[place])
             for place in range(places):
-                pick_ref[place * pack + quarter, pl.ds(pl.multiple_of(group * 8, 8), 8), :] = picks[place]
+                found[place].append(picks[place])
+        rows = pl.ds(pl.multiple_of(group * 8, 8), 8)
+        for place in range(places):
+            ranked = found[place]
+            if place == places // 2:
+                ranked = [jnp.where(pick == lane, LANES, pick) for pick in ranked]
+            for turn in range(pack):
+                for low in range(turn % 2, pack - 1, 2):
+                    pair = ranked[low], ranked[low + 1]
+                    ranked[low], ranked[low + 1] = jnp.minimum(*pair), jnp.maximum(*pair)
+            for level in range(pack):
+                pick_ref[level, place, rows, :] = ranked[level]
         return carry
 
-    lax.fori_loop(0, pick_ref.shape[1] // 8, group_picks, 0)
-
-
-def finish_kernel(bands, obs, list_len, rows, mix_ref, data_ref, own_ref, zp_two_ref, zp_own_ref, means_ref, misfit_ref):
+    lax.fori_loop(0, pick_ref.shape[2] // 8, group_picks, 0)
+
+
+def finish_kernel(
+    bands, obs, list_len, rows,
+    mix_ref, data_ref, data_places_ref, mags_ref, wts_ref, places_ref, zp_two_ref, zp_own_ref,
+    means_ref, misfit_ref,
+):
     halves = rows // LANES
     pack = LANES // list_len
-    mine = data_ref.shape[2] // rows
+    mine = data_ref.shape[3] // rows
     first = lax.rem(lax.axis_index("band") * mine, pack)
 
     def spread(row, picks):
-        table = jnp.broadcast_to(row, (obs, LANES))
-        return jnp.take_along_axis(table, picks, axis=1, mode="promise_in_bounds")
+        return take(jnp.broadcast_to(row, (obs, LANES)), picks)
 
     for block in range(zp_own_ref.shape[0] * pack):
         row = zp_own_ref[block // pack : block // pack + 1, :]
         for half in range(halves):
             cols = pl.ds(block * rows + half * LANES, LANES)
-            wts = own_ref[obs : 2 * obs, cols]
-            picks = own_ref[2 * obs : 3 * obs, cols].astype(jnp.int32) + block % pack * list_len
-            left = wts * (own_ref[0:obs, cols] - spread(row, picks))
+            wts = wts_ref[:, cols]
+            picks = places_ref[:, cols] + block % pack * list_len
+            left = wts * (mags_ref[:, cols] - spread(row, picks))
             means_ref[0:1, cols] = jnp.sum(left, axis=0, keepdims=True) / jnp.sum(wts, axis=0, keepdims=True)
 
     lines = []
@@ -352,17 +514,17 @@
                 cols = pl.ds(block * rows + half * LANES, LANES)
                 left, means = [], []
                 for band in range(bands):
-                    wts = data_ref[band, obs : 2 * obs, cols]
-                    picks = data_ref[band, 2 * obs : 3 * obs, cols].astype(jnp.int32) + (first + block) * list_len
+                    wts = data_ref[band, 1, :, cols]
+                    picks = data_places_ref[band, :, cols] + (first + block) * list_len
                     row = zp_two_ref[sweep, band]
-                    mags = data_ref[band, 0:obs, cols] - spread(row, picks)
+                    mags = data_ref[band, 0, :, cols] - spread(row, picks)
                     left.append(mags)
                     means.append(jnp.sum(wts * mags, axis=0, keepdims=True) / jnp.sum(wts, axis=0, keepdims=True))
                 for band in range(bands):
                     predicted = mix_ref[band, 0] * means[0]
                     for other in range(1, bands):
                         predicted = predicted + mix_ref[band, other] * means[other]
-                    wts = data_ref[band, obs : 2 * obs, cols]
+                    wts = data_ref[band, 1, :, cols]
                     partial[band] = partial[band] + wts * (left[band] - predicted) ** 2
         lines += [jnp.sum(partial[band], axis=0, keepdims=True) for band in range(bands)]
     lines.append(jnp.zeros((LANES - len(lines), LANES), jnp.float32))
@@ -392,26 +554,26 @@
     hbm = pl.BlockSpec(memory_space=pl.ANY)
 
     field_no = jnp.arange(fields, dtype=jnp.int32)[:, None]
-    flat_fields = block_fields.reshape(1, -1)
-    own_colors = jnp.sum(jnp.where(field_no == flat_fields, colors[:, None], 0), axis=0)
-    own_colors = jnp.where(flat_fields[0] < fields, own_colors, -1)
-    lists = jnp.stack([flat_fields[0], own_colors]).reshape(2 * tile_rows, LANES)
-    own = jnp.concatenate([magnitudes[0], weights[0], slots[0].astype(jnp.float32)], axis=0)
-    by_peer = own.reshape(3 * obs, bands, mine * rows).transpose(1, 0, 2)
-    peers = tiles + bands - 2
-    lists, data = pl.pallas_call(
-        functools.partial(exchange_kernel, tiles, bands),
+    copies = 3 * (bands - 1) + tiles - 1
+    lists, data, places, data_places = pl.pallas_call(
+        functools.partial(exchange_kernel, tiles, bands, list_len, fields),
         out_shape=(
-            jax.ShapeDtypeStruct((tiles,) + lists.shape, jnp.int32),
-            jax.ShapeDtypeStruct(by_peer.shape, jnp.float32),
+            jax.ShapeDtypeStruct((tiles, 2, tile_rows, LANES), jnp.int32),
+            jax.ShapeDtypeStruct((bands, 2, obs, mine * rows), jnp.float32),
+            jax.ShapeDtypeStruct((obs, stars), jnp.int32),
+            jax.ShapeDtypeStruct((bands, obs, mine * rows), jnp.int32),
         ),
-        in_specs=[vmem, vmem],
-        out_specs=(vmem, vmem),
-        scratch_shapes=[pltpu.SemaphoreType.DMA((peers,)), pltpu.SemaphoreType.DMA((peers,))],
+        in_specs=[vmem] * 5,
+        out_specs=(vmem,) * 4,
+        scratch_shapes=[
+            pltpu.VMEM((8, LANES), jnp.int32),
+            pltpu.VMEM((2, tile_rows, LANES), jnp.int32),
+            pltpu.SemaphoreType.DMA((copies,)),
+            pltpu.SemaphoreType.DMA((copies,)),
+        ],
         compiler_params=pltpu.CompilerParams(collective_id=0, has_side_effects=True),
         name="exchange",
-    )(lists, by_peer)
-    lists = lists.reshape(tiles, 2, tile_rows, LANES)
+    )(block_fields, colors.reshape(-1, LANES), magnitudes[0], weights[0], slots[0])
     all_fields = lists[:, 0].reshape(row_count, LANES)
     entry_colors = lists[:, 1].reshape(row_count, LANES)
 
@@ -419,20 +581,20 @@
     coupled = pl.pallas_call(
         functools.partial(couple_kernel, bands, obs, list_len, rows),
         out_shape=jax.ShapeDtypeStruct((bands // 2, LANES + EXTRA, LANES), jnp.float32),
-        in_specs=[smem, vmem, vmem],
+        in_specs=[smem, vmem, vmem, vmem],
         out_specs=vmem,
         name="couple",
-    )(mixing, mix_grid, data)
+    )(mixing, mix_grid, data, data_places)
     reach_rows = REACH * tile_rows + tile_rows - 1
     padded = jnp.concatenate([all_fields[-8:], all_fields, all_fields[:8]], axis=0)
-    places = 2 * reach_rows + 1
+    reach = 2 * reach_rows + 1
     everyone = (tiles // 2, 2, bands // 2, 2) + coupled.shape
     copies = tiles // 2 - 1 + 9
     coupled, pick = pl.pallas_call(
-        functools.partial(spread_kernel, tiles // 2, (list_len, fields, places)),
+        functools.partial(spread_kernel, tiles // 2, (list_len, fields, reach)),
         out_shape=(
             jax.ShapeDtypeStruct(everyone, jnp.float32),
-            jax.ShapeDtypeStruct((places * pack, row_count, LANES), jnp.int32),
+            jax.ShapeDtypeStruct((pack, reach, row_count, LANES), jnp.int32),
         ),
         in_specs=[vmem, vmem],
         out_specs=(vmem, vmem),
@@ -456,8 +618,10 @@
             pltpu.VMEM((bands, row_count + 16, LANES), jnp.float32),
             pltpu.VMEM(big, jnp.float32),
             pltpu.VMEM(big, jnp.float32),
+            pltpu.VMEM(big, jnp.float32),
             pltpu.VMEM((4, bands, LANES + EXTRA, LANES), jnp.float32),
             pltpu.SemaphoreType.DMA((4,)),
+            pltpu.SMEM((2 * COLORS + 1,), jnp.int32),
         ],
         compiler_params=pltpu.CompilerParams(vmem_limit_bytes=60 * 1024 * 1024),
         name="sweeps",
@@ -473,11 +637,12 @@
             jax.ShapeDtypeStruct((1, stars), jnp.float32),
             jax.ShapeDtypeStruct((8, LANES), jnp.float32),
         ),
-        in_specs=[smem, vmem, vmem, vmem, vmem],
+        in_specs=[smem] + [vmem] * 7,
         out_specs=(vmem, vmem),
         name="finish",
-    )(mixing, data, own, zp_two, zp_tile)
+    )(mixing, data, data_places, magnitudes[0], weights[0], places, zp_two, zp_tile)
     slab = (8, LANES)
+    peers = tiles + bands - 2
     total = pl.pallas_call(
         functools.partial(total_kernel, tiles, bands),
         out_shape=jax.ShapeDtypeStruct(slab, jnp.float32),

time: 147 us -> 124 us (0.84)
  Pallas kernels: 115 us -> 100 us
  other arithmetic: 15.1 us -> 10.2 us
  local copies, waits for them, and re-layouts: 9.13 us -> 7.06 us
    pallas_call x1, Pallas kernels: 48.5 us -> 33.7 us  [body(): pl.pallas_call(functools.partial(sweep_kernel, bands, list_len, row_count...]
    reduce_sum x1 -> x0, other arithmetic: 2.47 us -> none  [body(): jnp.sum(jnp.where(field_no == flat_fields, colors[:, None], 0), axis=0)]
    transpose x1 -> x0, other arithmetic: 1.56 us -> none  [body(): by_peer = own.reshape(3 * obs, bands, mine * rows).transpose(1, 0, 2)]
where the time goes in v1:
time: 124 us
  Pallas kernels  100 us (81%)
  other arithmetic  10.2 us (8%)
  local copies, waits for them, and re-layouts  7.06 us (6%)
  between operations  6.56 us (5%)
    pallas_call x1, Pallas kernels, body(): pl.pallas_call(functools.partial(spread_kernel, tiles // 2, (list_len, fi...  37 us
    pallas_call x1, Pallas kernels, body(): pl.pallas_call(functools.partial(sweep_kernel, bands, list_len, row_count...  33.7 us
    pallas_call x1, Pallas kernels, body(): pl.pallas_call(functools.partial(total_kernel, tiles, bands), out_shape=j...  12.9 us
    pallas_call x1, Pallas kernels, body(): pl.pallas_call(functools.partial(exchange_kernel, tiles, bands, list_len,...  11.9 us
    reduce_sum x1, other arithmetic, body(): jnp.sum((is_mine & (field_no == close_fields[None])).astype(jnp.int32), a...  4.08 us
    pallas_call x1, Pallas kernels, body(): pl.pallas_call(functools.partial(couple_kernel, bands, obs, list_len, row...  2.83 us

profile of v1, /device:TPU:0, one launch (start us, length us, event | category | flops | bytes accessed | tf_op | source)
XLA Modules:
  0.0 124.1 jit_solution(5036784987033445047)
XLA Ops:
  0.7 0.8 reduce_sum.38
  1.5 0.6 fusion.5
  7.9 1.3 %select_subtract_fusion.mix_ref = f32[4,4]{1,0:T(4,128)} fusion(f32[4,4]{1,0:T(4,128)} %param.13, f32[4]{0:T(128)S(1)} %reduce_sum.38), kind=kLoop, calls=%fused_computation.28 | loop fusion | flops 80 | bytes 144 | tf_op jit(solution)/shard_map/sub | solution.py:550
  9.2 0.8 fusion.6
  10.0 0.7 broadcast_compare_fusion
  10.7 0.1 broadcast_in_dim.72
  10.8 0.1 reshape.41
  10.9 0.7 copy.14.mix_grid_ref
  11.6 11.9 %exchange.1 = (s32[8,2,2,128]{3,2,1,0:T(2,128)}, f32[4,2,8,512]{3,2,1,0:T(8,128)}, s32[8,2048]{1,0:T(8,128)}, s32[4,8,512]{2,1,0:T(8,128)}) custom-call(s32[8,32]{1,0:T(8,128)} %lists_ref.1, s32[32,128]{1,0:T(8,128)} %bitcast.45, f32[8,2048]{1,0:T(8,128)} %bitcast.35, f32[8,2048]{1,0:T(8,128)} %bitcast.37, s32[8,2048]{1,0:T(8,128)} %bitcast.40), custom_call_target="tpu_custom_call" | custom-call | tf_op jit(solution)/shard_map/exchange/pallas_call | solution.py:558
  23.5 0.7 fusion.4
  24.2 1.3 %slice_bitcast_fusion = (s32[1,8,2,128]{3,2,1,0:T(2,128)S(1)}, s32[8,1,2,128]{3,2,1,0:T(2,128)}, s32[8,1,2,128]{3,2,1,0:T(2,128)S(1)}) fusion(s32[8,2,2,128]{3,2,1,0:T(2,128)} %get-tuple-element.11), kind=kLoop, calls=%fused_computation.34 | loop fusion | bytes 40960
  25.5 4.1 %convert_reduce_fusion.1 = (s32[768]{0:T(1024)S(1)}, s32[768]{0:T(1024)S(1)}) fusion(s32[768]{0:T(1024)S(1)} %pad_add_fusion.1, pred[4096]{0:T(1024)(128)(4,1)S(1)} %broadcast_compare_fusion), kind=kLoop, calls=%fused_computation.2 | loop fusion | flops 25164288 | bytes 13312 | tf_op jit(solution)/shard_map/reduce_sum | solution.py:674
  29.6 0.3 select_reduce_fusion.1
  29.9 0.6 pad_add_fusion.rows_ref
  30.5 2.8 %couple.1.own_ref = f32[2,136,128]{2,1,0:T(8,128)} custom-call(f32[4,4]{1,0:T(4,128)} %select_subtract_fusion.mix_ref, f32[128,128]{1,0:T(8,128)} %copy.14.mix_grid_ref, f32[4,2,8,512]{3,2,1,0:T(8,128)} %get-tuple-element.12.data_ref, s32[4,8,512]{2,1,0:T(8,128)} %get-tuple-element.13.places_ref.data_places_ref), custom_call_target="tpu_custom_call" | custom-call | tf_op jit(solution)/shard_map/couple/pallas_call | solution.py:581
  33.4 37.0 %spread.1 = (f32[4,2,2,2,2,136,128]{6,5,4,3,2,1,0:T(8,128)}, s32[4,11,16,128]{3,2,1,0:T(8,128)}) custom-call(f32[2,136,128]{2,1,0:T(8,128)} %couple.1.own_ref, s32[32,128]{1,0:T(8,128)} %pad_add_fusion.rows_ref), custom_call_target="tpu_custom_call" | custom-call | tf_op jit(solution)/shard_map/spread/pallas_call | solution.py:593
  70.4 33.7 %sweeps.1 = f32[4,4,16,128]{3,2,1,0:T(8,128)} custom-call(f32[64,136,128]{2,1,0:T(8,128)} %bitcast.34, s32[4,11,16,128]{3,2,1,0:T(8,128)} %get-tuple-element.15.pick_ref, s32[16,128]{1,0:T(8,128)} %bitcast.41), custom_call_target="tpu_custom_call" | custom-call | tf_op jit(solution)/shard_map/sweeps/pallas_call | solution.py:610
  104.1 1.5 %constant_dynamic-slice_fusion.2.zp_two_ref = f32[4,4,1,128]{3,2,1,0:T(1,128)} fusion(f32[4,4,16,128]{3,2,1,0:T(8,128)} %sweeps.1, s32[]{:T(128)S(6)} %select_n.71), kind=kLoop, calls=%fused_computation.18 | loop fusion | bytes 16388 | tf_op jit(solution)/shard_map/dynamic_slice | solution.py:633
  105.5 0.8 slice.49
  106.3 0.6 fusion.2.zp_own_ref
  106.9 2.0 %finish.1 = (f32[1,2048]{1,0:T(1,128)}, f32[8,128]{1,0:T(8,128)}) custom-call(f32[4,4]{1,0:T(4,128)} %select_subtract_fusion.mix_ref, f32[4,2,8,512]{3,2,1,0:T(8,128)} %get-tuple-element.12.data_ref, s32[4,8,512]{2,1,0:T(8,128)} %get-tuple-element.13.places_ref.data_places_ref, f32[8,2048]{1,0:T(8,128)} %bitcast.36, f32[8,2048]{1,0:T(8,128)} %bitcast.38, ...), custom_call_target="tpu_custom_call" | custom-call | tf_op jit(solution)/shard_map/finish/pallas_call | solution.py:634
  108.9 0.9 select_reduce_fusion
  109.8 12.9 %total.1 = f32[8,128]{1,0:T(8,128)} custom-call(f32[8,128]{1,0:T(8,128)} %get-tuple-element.18.part_ref), custom_call_target="tpu_custom_call" | custom-call | tf_op jit(solution)/shard_map/total/pallas_call | solution.py:646
  122.7 0.7 multiply_reduce_fusion
  123.4 0.1 div.17
  123.5 0.1 constant_dynamic-slice_fusion
  123.5 0.6 copy.15
  (10 shorter events, 0.1 us)
